TPU v7x, 512 devices: a whole 4x4x16 slice. The times are simulated.
512 devices in a mesh: fsdp: 64 (over z, x), tp: 8 (over y, core).
Axes of the slice: x: 4, y: 4, z: 16, core: 2. Of those that a mesh axis runs over, the one named last changes fastest.
Arguments:
- tokens: bfloat16 [2, 8192, 8192], P(None, 'fsdp', 'tp'), may hold values from -6 to 6
- frozen_weight: bfloat16 [8192, 2048], P('tp', 'fsdp'), may hold values from -0.0625 to 0.0625
- cotangent: bfloat16 [2, 8192, 2048], P(None, 'fsdp'), may hold values from -6 to 6
- block_adapter_index: int32 [2, 64], replicated, may hold values from 0 to 511
- down_weight: bfloat16 [512, 8192, 16], P(None, ('tp', 'fsdp')), may hold values from -0.0625 to 0.0625
- up_weight: bfloat16 [512, 16, 2048], P(None, None, ('tp', 'fsdp')), may hold values from -0.125 to 0.125
Outputs:
- key_value_output: bfloat16 [2, 8192, 2048], P(None, 'fsdp', 'tp')
- input_gradient: bfloat16 [2, 8192, 8192], P(None, 'fsdp', 'tp')
- grad_down: float32 [512, 8192, 16], P(None, ('tp', 'fsdp'))
- up_weight_gradient: float32 [512, 16, 2048], P(None, None, ('tp', 'fsdp'))
Inputs may be any that keep to these rules, and one draw needn't show every extreme that they name: `block_adapter_index`: one adapter for each block of 128 rows of a microbatch.
All inputs are finite; a program needn't handle non-finite values.
Results may differ from a plain program's by a relative error of at most 0.005.
Values may be sent and summed in bfloat16 or wider, within the bound.
A program may use at most 64 MiB of HBM per device.

v0:
```python
import jax
import jax.numpy as jnp
from jax import lax
from jax.sharding import Mesh
from jax.sharding import PartitionSpec as P

BLOCK = 128
FSDP = ("fsdp_0", "fsdp_1")
TP_FSDP = ("tp", "fsdp_0", "fsdp_1")


adapter_scale = 2.0


def gathered_by_axis(value, axes, dim):
    for axis in reversed(axes):
        value = lax.all_gather(value, axis, axis=dim, tiled=True)
    return value


def in_blocks(value, dim, devices):
    before, after = (value.shape[:dim], value.shape[dim + 1 :])
    return jnp.moveaxis(value.reshape(*before, devices, -1, *after), dim, 0)


def sent_and_summed(value, axis, dim):
    pieces = in_blocks(value, dim, lax.axis_size(axis))
    arrived = lax.all_to_all(pieces, axis, split_axis=0, concat_axis=0, tiled=True)
    return arrived.sum(axis=0)


def joined_along(pieces, dim):
    pieces = jnp.moveaxis(pieces, 0, dim)
    shape = pieces.shape
    return pieces.reshape(*shape[:dim], shape[dim] * shape[dim + 1], *shape[dim + 2 :])


def exchange_in_order(pieces, axes, turns):
    inside = pieces.shape[1:]
    out = pieces.reshape(*(lax.axis_size(a) for a in axes), *inside)
    for k in turns:
        out = lax.all_to_all(out, axes[k], k, k, tiled=True)
    return out.reshape(-1, *inside)


def stepwise_exchange(value, axes, turns, split_dim, concat_dim):
    pieces = in_blocks(value, split_dim, lax.axis_size(axes))
    return joined_along(exchange_in_order(pieces, axes, turns), concat_dim)


def sent_to_all(value, axis):
    devices = lax.axis_size(axis)
    return lax.all_to_all(
        jnp.broadcast_to(value[None], (devices, *value.shape)), axis, 0, 0, tiled=True
    )


def over_copies(value, axis):
    everything = sent_to_all(value, axis)
    return jnp.sum(everything, axis=0)


def packed_total(arrays, axis):
    line, at, finished = (jnp.concatenate([a.reshape(-1) for a in arrays]), 0, [])
    subtotal = over_copies(line, axis)
    for a in arrays:
        finished.append(subtotal[at : at + a.size].reshape(a.shape))
        at += a.size
    return tuple(finished)


def selected_sum(adapter_selector, tiles):
    flat = tiles.reshape(tiles.shape[0], -1)
    return lax.dot_general(
        adapter_selector,
        flat,
        (((0,), (0,)), ((), ())),
        precision=lax.Precision.HIGHEST,
        preferred_element_type=jnp.float32,
    )


def local(tokens, frozen_weight, cotangent, block_adapter_index, down_weight, up_weight):
    microbatch_list, token_block_rows, shard_width = tokens.shape
    kv_width = cotangent.shape[2]
    key_value_slice = kv_width // lax.axis_size("tp")
    row_total = microbatch_list * token_block_rows
    tok_matrix = tokens.reshape(row_total, shard_width)
    cot_matrix = cotangent.reshape(row_total, kv_width)
    adapter_number = down_weight.shape[0]
    rank_width = down_weight.shape[2]
    adapter_range = jnp.arange(adapter_number, dtype=jnp.int32)
    gathered = gathered_by_axis(frozen_weight, FSDP, 1)
    kv_partial = jnp.dot(tok_matrix, gathered, preferred_element_type=jnp.float32)
    frozen_key_value = sent_and_summed(kv_partial, "tp", 1)
    frozen_input_gradient = lax.dot_general(
        cot_matrix, gathered, (((1,), (1,)), ((), ())), preferred_element_type=jnp.float32
    )
    cot_slab = lax.dynamic_slice_in_dim(
        cotangent, lax.axis_index("tp") * key_value_slice, key_value_slice, 2
    )
    fsdp_count = lax.axis_size(FSDP)
    per_dev = token_block_rows // BLOCK
    dest_ids = (
        block_adapter_index.reshape(microbatch_list, fsdp_count, per_dev)
        .transpose(1, 0, 2)
        .reshape(fsdp_count, microbatch_list * per_dev)
    )
    down_send = jnp.take(down_weight, dest_ids, axis=0).transpose(0, 1, 3, 2)
    up_send = jnp.take(up_weight, dest_ids, axis=0)
    down_mine, up_mine = (
        stepwise_exchange(down_send, FSDP, (0, 1), 0, 3),
        stepwise_exchange(up_send, FSDP, (0, 1), 0, 3),
    )
    down_mine = down_mine.reshape(microbatch_list, per_dev, rank_width, shard_width)
    up_mine = up_mine.reshape(microbatch_list, per_dev, rank_width, key_value_slice)
    tok_blocks = tokens.reshape(microbatch_list, per_dev, BLOCK, shard_width)
    gradient_blocks = cot_slab.reshape(microbatch_list, per_dev, BLOCK, key_value_slice)
    low_part = jnp.einsum(
        "mnbc,mnrc->mnbr", tok_blocks, down_mine, preferred_element_type=jnp.float32
    )
    partial_input_gradient = adapter_scale * jnp.einsum(
        "fsvj,fsyj->fsvy", gradient_blocks, up_mine, preferred_element_type=jnp.float32
    )
    low_sum, back_sum = packed_total((low_part, partial_input_gradient), "tp")
    low_rank = low_sum.astype(jnp.bfloat16)
    rank_gradient = back_sum.astype(jnp.bfloat16)
    adapter_key_value = (
        adapter_scale
        * jnp.einsum("elui,elis->elus", low_rank, up_mine, preferred_element_type=jnp.float32)
    ).astype(jnp.bfloat16)
    adapter_input_gradient = jnp.einsum(
        "mnbr,mnrc->mnbc", rank_gradient, down_mine, preferred_element_type=jnp.float32
    ).astype(jnp.bfloat16)
    adapter_key_value = adapter_key_value.reshape(
        microbatch_list, token_block_rows, key_value_slice
    )
    adapter_input_gradient = adapter_input_gradient.reshape(
        microbatch_list, token_block_rows, shard_width
    )
    down_tiles = jnp.einsum(
        "mnbc,mnbr->mnrc", tok_blocks, rank_gradient, preferred_element_type=jnp.float32
    )
    up_weight_tiles = adapter_scale * jnp.einsum(
        "puai,puac->puic", low_rank, gradient_blocks, preferred_element_type=jnp.float32
    )
    down_tiles = down_tiles.reshape(microbatch_list * per_dev, rank_width, shard_width)
    up_weight_tiles = up_weight_tiles.reshape(
        microbatch_list * per_dev, rank_width, key_value_slice
    )
    down_owned, up_owned = (
        stepwise_exchange(down_tiles.astype(jnp.bfloat16), FSDP, (0, 1), 2, 0).astype(
            down_tiles.dtype
        ),
        stepwise_exchange(up_weight_tiles.astype(jnp.bfloat16), FSDP, (0, 1), 2, 0).astype(
            up_weight_tiles.dtype
        ),
    )
    owned_ids = dest_ids.reshape(-1)
    adapter_selector = (owned_ids[:, None] == adapter_range[None, :]).astype(jnp.float32)
    grad_down = (
        selected_sum(adapter_selector, down_owned)
        .reshape(adapter_number, rank_width, down_weight.shape[1])
        .transpose(0, 2, 1)
    )
    up_weight_gradient = selected_sum(adapter_selector, up_owned).reshape(up_weight.shape)
    key_value_output = (
        frozen_key_value.reshape(microbatch_list, token_block_rows, key_value_slice)
        + adapter_key_value.astype(jnp.float32)
    ).astype(jnp.bfloat16)
    input_gradient = (
        frozen_input_gradient.reshape(microbatch_list, token_block_rows, shard_width)
        + adapter_input_gradient.astype(jnp.float32)
    ).astype(jnp.bfloat16)
    return (key_value_output, input_gradient, grad_down, up_weight_gradient)


def solution(mesh):
    finer = Mesh(mesh.devices.reshape(16, 4, mesh.shape["tp"]), ("fsdp_0", "fsdp_1", "tp"))
    return jax.shard_map(
        local,
        mesh=finer,
        in_specs=(
            P(None, FSDP, "tp"),
            P("tp", FSDP),
            P(None, FSDP, None),
            P(),
            P(None, TP_FSDP, None),
            P(None, None, TP_FSDP),
        ),
        out_specs=(
            P(None, FSDP, "tp"),
            P(None, FSDP, "tp"),
            P(None, TP_FSDP, None),
            P(None, None, TP_FSDP),
        ),
        check_vma=False,
    )
```

profile of v0, /device:TPU:1, one launch (start us, length us, event | category | flops | bytes accessed | tf_op | source)
XLA Modules:
  0.0 201.9 jit_solution(8756875454586516329)
XLA Ops:
  7.2 10.9 %all_gather.6 = bf16[1024,128]{0,1:T(8,128)(2,1)S(1)} all-gather(bf16[1024,32]{0,1:T(8,128)(2,1)} %param.7), channel_id=1, replica_groups=mesh['fsdp_0'=16,'fsdp_1'=4,'tp'=8] {'fsdp_1'}, dimensions={1}, use_global_device_ids=true | all-gather | bytes 327680 | tf_op jit(solution)/shard_map/all_gather | solution.py:17
  18.1 0.8 copy.190
  19.0 0.7 compare_select_fusion
  19.9 1.3 copy.201
  21.2 0.7 gather_fusion.1
  21.9 0.7 compare_and_fusion
  22.8 0.2 copy_bitcast_fusion.5
  23.0 0.8 reshape.193
  23.7 15.4 %all-to-all-start.3 = ((bf16[16,2,256]{2,1,0:T(2,128)(2,1)}), bf16[16,2,256]{2,1,0:T(2,128)(2,1)S(1)}, u32[]{:S(2)}, u32[]{:S(2)}) async-start(bf16[16,2,256]{2,1,0:T(2,128)(2,1)} %reshape.193), calls=%async_computation.3 | async-start | bytes 32768 | tf_op jit(solution)/shard_map/all_to_all | solution.py:42
  39.1 0.7 fusion.40
  39.8 2.8 %copy.194 = bf16[512,16,16]{2,1,0:T(8,128)(2,1)S(1)} copy(bf16[512,16,16]{0,2,1:T(8,128)(2,1)} %param.10) | data formatting | bytes 524288 | tf_op args[4]
  42.6 1.5 gather_fusion
  44.2 6.4 %all-to-all-done.3 = bf16[16,2,256]{2,1,0:T(2,128)(2,1)S(1)} async-done(((bf16[16,2,256]{2,1,0:T(2,128)(2,1)}), bf16[16,2,256]{2,1,0:T(2,128)(2,1)S(1)}, u32[]{:S(2)}, u32[]{:S(2)}) %all-to-all-start.3) | async-done | bytes 16416 | tf_op jit(solution)/shard_map/all_to_all | solution.py:42
  50.9 0.8 reshape.195
  51.6 3.3 %all-to-all-start.4 = ((bf16[4,2,1024]{2,1,0:T(2,128)(2,1)}), bf16[4,2,1024]{2,1,0:T(2,128)(2,1)S(1)}, u32[]{:S(2)}, u32[]{:S(2)}) async-start(bf16[4,2,1024]{2,1,0:T(2,128)(2,1)} %reshape.195), calls=%async_computation.4 | async-start | bytes 32768 | tf_op jit(solution)/shard_map/all_to_all | solution.py:42
  54.9 1.3 broadcast_select_fusion
  56.2 1.2 reshape.197
  57.4 1.7 all-to-all-done.4
  59.1 5.0 %all-to-all-start.1 = ((bf16[16,2,1024]{2,1,0:T(2,128)(2,1)}), bf16[16,2,1024]{2,1,0:T(2,128)(2,1)S(1)}, u32[]{:S(2)}, u32[]{:S(2)}) async-start(bf16[16,2,1024]{2,1,0:T(2,128)(2,1)} %reshape.197), calls=%async_computation.1 | async-start | bytes 131072 | tf_op jit(solution)/shard_map/all_to_all | solution.py:42
  64.5 11.4 %all-to-all-done.1 = bf16[16,2,1024]{2,1,0:T(2,128)(2,1)S(1)} async-done(((bf16[16,2,1024]{2,1,0:T(2,128)(2,1)}), bf16[16,2,1024]{2,1,0:T(2,128)(2,1)S(1)}, u32[]{:S(2)}, u32[]{:S(2)}) %all-to-all-start.1) | async-done | bytes 65568 | tf_op jit(solution)/shard_map/all_to_all | solution.py:42
  76.0 0.4 reshape.198
  76.4 1.2 reshape.199
  77.6 3.3 %all-to-all-start.2 = ((bf16[4,2,4096]{2,1,0:T(2,128)(2,1)}), bf16[4,2,4096]{2,1,0:T(2,128)(2,1)S(1)}, u32[]{:S(2)}, u32[]{:S(2)}) async-start(bf16[4,2,4096]{2,1,0:T(2,128)(2,1)} %reshape.199), calls=%async_computation.2 | async-start | bytes 131072 | tf_op jit(solution)/shard_map/all_to_all | solution.py:42
  80.9 0.2 convolution_multiply_fusion.2
  81.3 4.0 %all-to-all-done.2 = bf16[4,2,4096]{2,1,0:T(2,128)(2,1)S(1)} async-done(((bf16[4,2,4096]{2,1,0:T(2,128)(2,1)}), bf16[4,2,4096]{2,1,0:T(2,128)(2,1)S(1)}, u32[]{:S(2)}, u32[]{:S(2)}) %all-to-all-start.2) | async-done | bytes 65568 | tf_op jit(solution)/shard_map/all_to_all | solution.py:42
  85.3 0.4 reshape.200
  85.7 0.3 copy.197
  85.9 0.2 copy.198
  86.2 0.8 reshape.162
  86.9 0.2 convolution_bitcast_fusion.2
  87.5 19.5 %all_to_all.51 = f32[8,1,8192]{2,1,0:T(1,128)S(1)} all-to-all(f32[8,1,8192]{2,1,0:T(1,128)S(1)} %broadcast_in_dim.34), channel_id=1, replica_groups=mesh['fsdp_0'=16,'fsdp_1'=4,'tp'=8] {'tp'}, dimensions={0} | all-to-all | bytes 524288 | tf_op jit(solution)/shard_map/all_to_all | solution.py:53
  107.0 0.2 reduce_sum.19
  107.4 0.2 fusion.13
  107.7 0.8 reshape.205
  108.5 3.5 %all-to-all-start.8 = ((bf16[16,2,256]{2,1,0:T(2,128)(2,1)}), bf16[16,2,256]{2,1,0:T(2,128)(2,1)S(1)}, u32[]{:S(2)}, u32[]{:S(2)}) async-start(bf16[16,2,256]{2,1,0:T(2,128)(2,1)} %reshape.205), calls=%async_computation.8 | async-start | bytes 32768 | tf_op jit(solution)/shard_map/all_to_all | solution.py:42
  112.1 0.2 convolution_convert_fusion.1
  112.3 0.4 convert_element_type.56
  112.8 0.3 copy.215
  113.1 1.2 reshape.201
  114.3 9.0 %all-to-all-done.8 = bf16[16,2,256]{2,1,0:T(2,128)(2,1)S(1)} async-done(((bf16[16,2,256]{2,1,0:T(2,128)(2,1)}), bf16[16,2,256]{2,1,0:T(2,128)(2,1)S(1)}, u32[]{:S(2)}, u32[]{:S(2)}) %all-to-all-start.8) | async-done | bytes 16416 | tf_op jit(solution)/shard_map/all_to_all | solution.py:42
  123.3 3.5 %all-to-all-start.6 = ((bf16[16,2,1024]{2,1,0:T(2,128)(2,1)}), bf16[16,2,1024]{2,1,0:T(2,128)(2,1)S(1)}, u32[]{:S(2)}, u32[]{:S(2)}) async-start(bf16[16,2,1024]{2,1,0:T(2,128)(2,1)} %reshape.201), calls=%async_computation.6 | async-start | bytes 131072 | tf_op jit(solution)/shard_map/all_to_all | solution.py:42
  127.0 0.8 reshape.207
  127.8 10.7 %all-to-all-done.6 = bf16[16,2,1024]{2,1,0:T(2,128)(2,1)S(1)} async-done(((bf16[16,2,1024]{2,1,0:T(2,128)(2,1)}), bf16[16,2,1024]{2,1,0:T(2,128)(2,1)S(1)}, u32[]{:S(2)}, u32[]{:S(2)}) %all-to-all-start.6) | async-done | bytes 65568 | tf_op jit(solution)/shard_map/all_to_all | solution.py:42
  138.5 3.3 %all-to-all-start.9 = ((bf16[4,2,1024]{2,1,0:T(2,128)(2,1)}), bf16[4,2,1024]{2,1,0:T(2,128)(2,1)S(1)}, u32[]{:S(2)}, u32[]{:S(2)}) async-start(bf16[4,2,1024]{2,1,0:T(2,128)(2,1)} %reshape.207), calls=%async_computation.9 | async-start | bytes 32768 | tf_op jit(solution)/shard_map/all_to_all | solution.py:42
  141.7 0.4 reshape.202
  142.1 1.2 reshape.203
  143.3 6.4 %copy.191 = bf16[2048,1024]{1,0:T(8,128)(2,1)} copy(bf16[2048,1024]{0,1:T(8,128)(2,1)} %bitcast.111) | data formatting | bytes 8388608 | tf_op jit(solution)/shard_map/dot_general | solution.py:94
  149.8 4.2 %all-to-all-start.7 = ((bf16[4,2,4096]{2,1,0:T(2,128)(2,1)}), bf16[4,2,4096]{2,1,0:T(2,128)(2,1)S(1)}, u32[]{:S(2)}, u32[]{:S(2)}) async-start(bf16[4,2,4096]{2,1,0:T(2,128)(2,1)} %reshape.203), calls=%async_computation.7 | async-start | bytes 131072 | tf_op jit(solution)/shard_map/all_to_all | solution.py:42
  154.0 4.9 %convolution_bitcast_fusion = f32[8,256,256]{2,1,0:T(8,128)} fusion(bf16[256,1024,1]{1,0,2:T(8,128)(2,1)S(1)} %bitcast.113, bf16[8,256,1024]{2,1,0:T(8,128)(2,1)} %bitcast.112), kind=kOutput, calls=%fused_computation.4 | convolution fusion | flops 1073741824 | bytes 6815744 | tf_op jit(solution)/shard_map/dot_general | solution.py:94
  158.8 8.1 %all-to-all-start = ((f32[8,256,256]{2,1,0:T(8,128)}), f32[8,256,256]{2,1,0:T(8,128)S(1)}, u32[]{:S(2)}, u32[]{:S(2)}) async-start(f32[8,256,256]{2,1,0:T(8,128)} %convolution_bitcast_fusion), calls=%async_computation | async-start | bytes 4194304 | tf_op jit(solution)/shard_map/all_to_all | solution.py:28
  167.2 1.3 fusion.8
  168.6 1.6 copy.223
  170.2 1.5 reshape.170
  171.8 0.3 fusion.15
  172.1 0.7 copy.227
  172.8 1.2 reshape.204
  174.0 1.9 copy.217
  175.9 1.5 reshape.168
  177.5 0.3 convolution_bitcast_fusion.1
  177.8 1.1 copy.226
  178.9 4.6 %fusion.5 = bf16[2,128,1024]{2,1,0:T(8,128)(2,1)} fusion(f32[2,128,1024]{2,1,0:T(8,128)} %fusion.8, bf16[2,128,2048]{2,1,0:T(8,128)(2,1)S(1)} %copy-done, bf16[1024,2048]{1,0:T(8,128)(2,1)} %all-gather.2.cloned.1.call-done), kind=kOutput, calls=%fused_computation.6 | convolution fusion | flops 1074266112 | bytes 6815744 | tf_op jit(solution)/shard_map/dot_general | solution.py:96
  183.5 9.7 %all-to-all-done = f32[8,256,256]{2,1,0:T(8,128)S(1)} async-done(((f32[8,256,256]{2,1,0:T(8,128)}), f32[8,256,256]{2,1,0:T(8,128)S(1)}, u32[]{:S(2)}, u32[]{:S(2)}) %all-to-all-start) | async-done | bytes 2097184 | tf_op jit(solution)/shard_map/all_to_all | solution.py:28
  193.2 0.1 reduce_sum.18
  193.3 1.7 fusion.12
  (44 shorter events, 2.9 us)
Async XLA Ops:
  7.2 73.7 %copy-start = (bf16[2,128,2048]{2,1,0:T(8,128)(2,1)S(1)}, bf16[2,128,2048]{2,1,0:T(8,128)(2,1)}, u32[]{:S(2)}) copy-start(bf16[2,128,2048]{2,1,0:T(8,128)(2,1)} %param.8) | copy-start | bytes 3145732
  7.2 136.1 %all-gather.2.cloned.1.call-start = ((), (), s32[]{:S(2)}) async-start(), calls=%async_computation.10 | async-start | bytes 4456448 | tf_op jit(solution)/shard_map/all_gather | solution.py:17
  23.7 26.9 %all-to-all-start.3 = ((bf16[16,2,256]{2,1,0:T(2,128)(2,1)}), bf16[16,2,256]{2,1,0:T(2,128)(2,1)S(1)}, u32[]{:S(2)}, u32[]{:S(2)}) async-start(bf16[16,2,256]{2,1,0:T(2,128)(2,1)} %reshape.193), calls=%async_computation.3 | async-start | bytes 32768 | tf_op jit(solution)/shard_map/all_to_all | solution.py:42
  51.6 7.5 %all-to-all-start.4 = ((bf16[4,2,1024]{2,1,0:T(2,128)(2,1)}), bf16[4,2,1024]{2,1,0:T(2,128)(2,1)S(1)}, u32[]{:S(2)}, u32[]{:S(2)}) async-start(bf16[4,2,1024]{2,1,0:T(2,128)(2,1)} %reshape.195), calls=%async_computation.4 | async-start | bytes 32768 | tf_op jit(solution)/shard_map/all_to_all | solution.py:42
  54.9 32.0 %copy-start.1 = (bf16[2,128,1024]{2,1,0:T(8,128)(2,1)S(1)}, bf16[2,128,1024]{2,1,0:T(8,128)(2,1)}, u32[]{:S(2)}) copy-start(bf16[2,128,1024]{2,1,0:T(8,128)(2,1)} %param.6) | copy-start | bytes 1572868
  59.1 16.8 %all-to-all-start.1 = ((bf16[16,2,1024]{2,1,0:T(2,128)(2,1)}), bf16[16,2,1024]{2,1,0:T(2,128)(2,1)S(1)}, u32[]{:S(2)}, u32[]{:S(2)}) async-start(bf16[16,2,1024]{2,1,0:T(2,128)(2,1)} %reshape.197), calls=%async_computation.1 | async-start | bytes 131072 | tf_op jit(solution)/shard_map/all_to_all | solution.py:42
  77.6 7.7 %all-to-all-start.2 = ((bf16[4,2,4096]{2,1,0:T(2,128)(2,1)}), bf16[4,2,4096]{2,1,0:T(2,128)(2,1)S(1)}, u32[]{:S(2)}, u32[]{:S(2)}) async-start(bf16[4,2,4096]{2,1,0:T(2,128)(2,1)} %reshape.199), calls=%async_computation.2 | async-start | bytes 131072 | tf_op jit(solution)/shard_map/all_to_all | solution.py:42
  107.4 4.8 %copy-start.2 = (bf16[2,128,16]{2,1,0:T(8,128)(2,1)}, bf16[2,128,16]{2,1,0:T(8,128)(2,1)S(1)}, u32[]{:S(2)}) copy-start(bf16[2,128,16]{2,1,0:T(8,128)(2,1)S(1)} %convert_element_type.47) | copy-start | bytes 24580
  108.5 14.8 %all-to-all-start.8 = ((bf16[16,2,256]{2,1,0:T(2,128)(2,1)}), bf16[16,2,256]{2,1,0:T(2,128)(2,1)S(1)}, u32[]{:S(2)}, u32[]{:S(2)}) async-start(bf16[16,2,256]{2,1,0:T(2,128)(2,1)} %reshape.205), calls=%async_computation.8 | async-start | bytes 32768 | tf_op jit(solution)/shard_map/all_to_all | solution.py:42
  123.3 15.1 %all-to-all-start.6 = ((bf16[16,2,1024]{2,1,0:T(2,128)(2,1)}), bf16[16,2,1024]{2,1,0:T(2,128)(2,1)S(1)}, u32[]{:S(2)}, u32[]{:S(2)}) async-start(bf16[16,2,1024]{2,1,0:T(2,128)(2,1)} %reshape.201), calls=%async_computation.6 | async-start | bytes 131072 | tf_op jit(solution)/shard_map/all_to_all | solution.py:42
  138.5 11.3 %all-to-all-start.9 = ((bf16[4,2,1024]{2,1,0:T(2,128)(2,1)}), bf16[4,2,1024]{2,1,0:T(2,128)(2,1)S(1)}, u32[]{:S(2)}, u32[]{:S(2)}) async-start(bf16[4,2,1024]{2,1,0:T(2,128)(2,1)} %reshape.207), calls=%async_computation.9 | async-start | bytes 32768 | tf_op jit(solution)/shard_map/all_to_all | solution.py:42
  149.8 9.1 %all-to-all-start.7 = ((bf16[4,2,4096]{2,1,0:T(2,128)(2,1)}), bf16[4,2,4096]{2,1,0:T(2,128)(2,1)S(1)}, u32[]{:S(2)}, u32[]{:S(2)}) async-start(bf16[4,2,4096]{2,1,0:T(2,128)(2,1)} %reshape.203), calls=%async_computation.7 | async-start | bytes 131072 | tf_op jit(solution)/shard_map/all_to_all | solution.py:42
  154.0 13.0 %copy-start.3 = (s32[2,64]{1,0:T(2,128)S(1)}, s32[2,64]{1,0:T(2,128)}, u32[]{:S(2)}) copy-start(s32[2,64]{1,0:T(2,128)} %param.9) | copy-start | bytes 1540
  158.8 34.3 %all-to-all-start = ((f32[8,256,256]{2,1,0:T(8,128)}), f32[8,256,256]{2,1,0:T(8,128)S(1)}, u32[]{:S(2)}, u32[]{:S(2)}) async-start(f32[8,256,256]{2,1,0:T(8,128)} %convolution_bitcast_fusion), calls=%async_computation | async-start | bytes 4194304 | tf_op jit(solution)/shard_map/all_to_all | solution.py:28
Sparse Core Ops, SparseCore 0:
  19.1 94.6 all-gather.1
where the time goes:
time: 203 us; the launch traced here: 202 us
  waiting for transfers between devices  53 us (26%)
  starting transfers between devices  49.5 us (24%)
  local copies, waits for them, and re-layouts  36.9 us (18%)
  blocking collectives  30.4 us (15%)
  between operations  14.4 us (7%)
  matrix products  13.8 us (7%)
  other arithmetic  3.95 us (2%)
    all_to_all x8, waiting for transfers between devices, exchange_in_order(): out = lax.all_to_all(out, axes[k], k, k, tiled=True)  43.2 us
    all_to_all x8, starting transfers between devices, exchange_in_order(): out = lax.all_to_all(out, axes[k], k, k, tiled=True)  41.4 us
    all_to_all x1, blocking collectives, sent_to_all(): lax.all_to_all(jnp.broadcast_to(value[None], (devices, *value.shape)), ax...  19.5 us
    unnamed x30, local copies, waits for them, and re-layouts  16.7 us
    all_gather x1, blocking collectives, gathered_by_axis(): value = lax.all_gather(value, axis, axis=dim, tiled=True)  10.9 us
    all_to_all x1, waiting for transfers between devices, sent_and_summed(): lax.all_to_all(pieces, axis, split_axis=0, concat_axis=0, tiled=True)  9.71 us
    all_to_all x1, starting transfers between devices, sent_and_summed(): lax.all_to_all(pieces, axis, split_axis=0, concat_axis=0, tiled=True)  8.11 us
    dot_general x1, local copies, waits for them, and re-layouts, local(): jnp.dot(tok_matrix, gathered, preferred_element_type=jnp.float32)  6.44 us
  transfers between devices with their start and end apart: 10, of which 7 were waited for; matrix products, arithmetic and copies ran while one was open for 26% of the time, Pallas kernels for 0%

commit v1 on v0

v1 whole, which is shorter than its diff:
```python
import functools

import jax
import jax.numpy as jnp
from jax import lax
from jax.experimental import pallas as pl
from jax.experimental.pallas import tpu as pltpu
from jax.sharding import Mesh
from jax.sharding import PartitionSpec as P

MESH = pl.DeviceIdType.MESH
PLANE = ("z", "x")
TP = ("y", "c")
ALL = ("y", "c", "z", "x")

ZN, XN, TN = 16, 4, 8
FN = ZN * XN
BF = jnp.bfloat16
F32 = jnp.float32
NA = 2
LA = NA * 128
LB = 1024 - LA
ADAPT_AT = 3
TILES_AT = 5


def nt(a, b):
    return lax.dot_general(a, b, (((1,), (1,)), ((), ())), preferred_element_type=F32)


def nn(a, b):
    return jnp.dot(a, b, preferred_element_type=F32)


def iota(shape, dim):
    return lax.broadcasted_iota(jnp.int32, shape, dim)


def kernel(
    tok_ref, wt_ref, cot_ref, idx_ref, dn_ref, up_ref,
    kv_ref, ig_ref, gd_ref, gu_ref,
    wa, wb, acc, own_kv, rs_send, rs_recv, kvl, igl,
    onehot, sb32, sb1, sb2, rb32, rb1, rb2, d2t, up2, ar_send, ar_recv,
    s_loc, s_a, r_a, s_ax, r_ax, s_b, r_b, s_bx, r_bx, s_bf, r_bf,
    s_rs, r_rs, s_ar, r_ar, s_e, r_e, l_e,
):
    z, x = lax.axis_index("z"), lax.axis_index("x")
    tp = lax.axis_index("y") * 2 + lax.axis_index("c")
    f = z * XN + x

    def zmod(v):
        return lax.rem(v + 4 * ZN, ZN)

    def xmod(v):
        return lax.rem(v + 4 * XN, XN)

    def remote(src, dst, send, recv, device):
        return pltpu.make_async_remote_copy(
            src_ref=src, dst_ref=dst, send_sem=send, recv_sem=recv,
            device_id=device, device_id_type=MESH,
        )

    def plane_device(q):
        return {"z": lax.div(q, XN), "x": lax.rem(q, XN)}

    def tp_device(q):
        return {"y": lax.div(q, 2), "c": lax.rem(q, 2)}

    def rows_at(base, size):
        return pl.ds(pl.multiple_of(base, size), size)

    barrier = pltpu.get_barrier_semaphore()

    @pl.loop(1, FN)
    def _(p):
        pl.semaphore_signal(
            barrier, 1, device_id=plane_device(lax.rem(f + p, FN)), device_id_type=MESH
        )

    @pl.loop(1, TN)
    def _(t):
        pl.semaphore_signal(
            barrier, 1, device_id=tp_device(lax.rem(tp + t, TN)), device_id_type=MESH
        )

    own_rows = rows_at(f * 32, 32)
    own_a = pltpu.make_async_copy(wt_ref.at[:, 0:LA], wa.at[own_rows], s_loc.at[0])
    own_b = pltpu.make_async_copy(wt_ref.at[:, LA:1024], wb.at[own_rows], s_loc.at[1])
    own_a.start()
    own_b.start()

    zeros_up = jnp.zeros((64, FN), F32)
    sb32[...] = jnp.zeros_like(sb32)
    for m in range(2):
        pick = jnp.where(iota((512, FN), 0) == idx_ref[m : m + 1, :], 1.0, 0.0).astype(BF)
        onehot[m] = pick
        down = jnp.transpose(nn(dn_ref[...], pick))
        sb32[:, 2 * m, :] = down[:, 0:128]
        sb32[:, 2 * m + 1, :] = down[:, 128:256]
        up = jnp.concatenate([nn(up_ref[...], pick), zeros_up], axis=0)
        sb32[:, 4 + m, :] = jnp.transpose(up)
    sb1[...] = sb32[...].astype(BF)

    own_a.wait()
    own_b.wait()
    pl.semaphore_wait(barrier, FN - 1 + TN - 1)

    def exchange_start(src, dst, n):
        own = pltpu.make_async_copy(src.at[f], dst.at[f], l_e.at[n])
        own.start()

        @pl.loop(1, FN)
        def _(p):
            q = lax.rem(f + p, FN)
            remote(src.at[q], dst.at[f], s_e.at[n], r_e.at[n], plane_device(q)).start()

    def exchange_wait(src, dst, n):
        pltpu.make_async_copy(src.at[f], dst.at[f], l_e.at[n]).wait()
        remote(
            src.at[0 : FN - 1], dst.at[0 : FN - 1], s_e.at[n], r_e.at[n], plane_device(f)
        ).wait_recv()

    def exchange_drain(src, dst, n):
        remote(
            src.at[0 : FN - 1], dst.at[0 : FN - 1], s_e.at[n], r_e.at[n], plane_device(f)
        ).wait_send()

    def a_rows(d, k, xs):
        zz = zmod(z - k) if d == 0 else zmod(z + k)
        return rows_at(zz * 128 + xs * 32, 32)

    def b_rows(d, k):
        return a_rows(d, k, x)

    def ring_device(d):
        return {"z": zmod(z + 1) if d == 0 else zmod(z - 1)}

    def a_copy(d, k, xs):
        rows = wa.at[a_rows(d, k, xs)]
        return remote(rows, rows, s_a.at[d, k, xs], r_a.at[d, k + 1, xs], ring_device(d))

    def a_wait(d, k, xs):
        rows = wa.at[a_rows(d, k, xs)]
        remote(rows, rows, s_a.at[d, 0, xs], r_a.at[d, k, xs], ring_device(d)).wait_recv()

    def ax_copy(i):
        rows = wa.at[own_rows]
        return remote(rows, rows, s_ax.at[i], r_ax.at[x], {"x": xmod(x + i)})

    def ax_wait(xs):
        rows = wa.at[a_rows(0, 0, xs)]
        remote(rows, rows, s_ax.at[1], r_ax.at[xs], {"x": xmod(x + 1)}).wait_recv()

    def b_copy(d, k):
        rows = wb.at[b_rows(d, k)]
        return remote(rows, rows, s_b.at[d, k], r_b.at[d, k + 1], ring_device(d))

    def b_wait(d, k):
        rows = wb.at[b_rows(d, k)]
        remote(rows, rows, s_b.at[d, 0], r_b.at[d, k], ring_device(d)).wait_recv()

    def b_half(d, k):
        zz = zmod(z - k) if d == 0 else zmod(z + k)
        return wb.at[rows_at(zz * 128 + x * 32 + 16 * d, 16)]

    def b_half_copy(d):
        rows = b_half(d, 7)
        return remote(rows, rows, s_b.at[d, 7], r_b.at[d, 8], ring_device(d))

    def b_half_wait(d):
        rows = b_half(d, 8)
        remote(rows, rows, s_b.at[d, 7], r_b.at[d, 8], ring_device(d)).wait_recv()

    def slot(d, k):
        return k if d == 0 else 8 + k

    def x_device(side):
        return {"x": xmod(x + 1)} if side == 0 else {"x": xmod(x - 1)}

    def bx_rows(d, k, from_x):
        return wb.at[a_rows(d, k, from_x)]

    def bx_copy(side, d, k):
        rows = bx_rows(d, k, x)
        n = slot(d, k)
        return remote(rows, rows, s_bx.at[side, n], r_bx.at[side, n], x_device(side))

    def bx_wait(side, d, k):
        n = slot(d, k)
        rows = bx_rows(d, k, xmod(x - 1) if side == 0 else xmod(x + 1))
        remote(rows, rows, s_bx.at[side, n], r_bx.at[side, n], x_device(side)).wait_recv()

    def bf_rows(side, d, k, from_x):
        zz = zmod(z - k) if d == 0 else zmod(z + k)
        return wb.at[rows_at(zz * 128 + from_x * 32 + 16 * side, 16)]

    def bf_copy(side, d, k):
        n = slot(d, k)
        rows = bf_rows(side, d, k, xmod(x - 1) if side == 0 else xmod(x + 1))
        return remote(rows, rows, s_bf.at[side, n], r_bf.at[side, n], x_device(side))

    def bf_wait(side, d, k):
        n = slot(d, k)
        rows = bf_rows(side, d, k, xmod(x + 2))
        remote(rows, rows, s_bf.at[side, n], r_bf.at[side, n], x_device(side)).wait_recv()

    def spread(d, k):
        for side in range(2):
            bx_copy(side, d, k).start()

    def forward_x(d, k):
        for side in range(2):
            bx_wait(side, d, k)
            bf_copy(side, d, k).start()

    def complete_x(d, k):
        for side in range(2):
            bf_wait(side, d, k)

    def rs_copy(c):
        return remote(
            rs_send.at[c], rs_recv.at[tp], s_rs.at[c], r_rs.at[tp], tp_device(c)
        )

    def block(k):
        odd = lax.rem(z + k, 2)
        start = zmod(jnp.where(odd == 1, z + k - 1, z - k))
        c = lax.div(start, 2)
        rows = rows_at(c * 256, 256)
        w_a, w_b = wa[rows, :], wb[rows, :]
        part = nt(tok_ref[:, 0:LA], w_a) + nt(tok_ref[:, LA:1024], w_b)

        @pl.when(c == tp)
        def _():
            own_kv[...] = part

        @pl.when(c != tp)
        def _():
            rs_send[c] = part.astype(BF)
            rs_copy(c).start()

        cot = cot_ref[:, rows]
        acc[:, 0:LA] += nn(cot, w_a)
        acc[:, LA:1024] += nn(cot, w_b)

    rep = jnp.where(lax.div(iota((FN, 1024), 1), 16) == iota((FN, 1024), 0), 1.0, 0.0).astype(BF)
    rep_up = jnp.where(lax.div(iota((FN, 256), 1), 4) == iota((FN, 256), 0), 1.0, 0.0).astype(BF)
    lane16 = lax.rem(iota((16, 1024), 1), 16)
    lane4 = lax.rem(iota((16, 256), 1), 4)
    first = iota((16, 256), 1) < 128
    cot_cols = pl.ds(pl.multiple_of(tp * 256, 256), 256)

    def arrived(m):
        down = jnp.concatenate(
            [jnp.transpose(rb32[:, 2 * m, :]), jnp.transpose(rb32[:, 2 * m + 1, :])], axis=0
        )
        up = jnp.transpose(rb32[:, 4 + m, :])[0:64, :]
        return down.astype(BF), up.astype(BF)

    def folded(value):
        return jnp.where(first, value[0:16], value[16:32])

    def unfolded(value):
        return jnp.concatenate(
            [jnp.where(first, value, 0.0), jnp.where(first, 0.0, value)], axis=0
        )

    def adapters():
        exchange_wait(sb1, rb1, 0)
        rb32[...] = rb1[...].astype(F32)
        for m in range(2):
            down, up = arrived(m)
            wide = nn(down, rep)
            total = jnp.zeros((16, 1024), F32)
            for d in range(16):
                total = jnp.where(lane16 == d, wide[16 * d : 16 * d + 16], total)
            d2t[16 * m : 16 * m + 16] = total.astype(BF)
            wide = nn(up, rep_up)
            total = jnp.zeros((16, 256), F32)
            for d in range(4):
                total = jnp.where(lane4 == d, wide[16 * d : 16 * d + 16], total)
            up2[16 * m : 16 * m + 16] = total.astype(BF)
        ar_send[0:16] = folded(nt(d2t[...], tok_ref[...]))
        ar_send[16:32] = 2.0 * folded(nt(up2[...], cot_ref[:, cot_cols]))
        ar_recv[tp] = ar_send[...]

        @pl.loop(1, TN)
        def _(t):
            ar_copy(t).start()

    def ar_copy(t):
        q = lax.rem(tp + t, TN)
        return remote(ar_send, ar_recv.at[tp], s_ar.at[t], r_ar.at[tp], tp_device(q))

    def tiles():
        @pl.loop(1, TN)
        def _(t):
            q = lax.rem(tp + t, TN)
            remote(ar_send, ar_recv.at[q], s_ar.at[t], r_ar.at[q], tp_device(q)).wait_recv()

        total = ar_recv[0]
        for q in range(1, TN):
            total = total + ar_recv[q]
        low = unfolded(total[0:16].astype(BF).astype(F32))
        back = unfolded(total[16:32].astype(BF).astype(F32))
        low_t, back_t = jnp.transpose(low).astype(BF), jnp.transpose(back).astype(BF)
        low, back = low.astype(BF), back.astype(BF)
        down = nn(back, tok_ref[...])
        up = 2.0 * nn(low, cot_ref[:, cot_cols])
        zeros = jnp.zeros((64, 256), BF)
        for m in range(2):
            mine = down[16 * m : 16 * m + 16]
            wide = jnp.concatenate(
                [jnp.where(lane16 == d, mine, 0.0).astype(BF) for d in range(16)], axis=0
            )
            packed = jnp.transpose(nt(wide, rep))
            sb32[:, 2 * m, :] = packed[:, 0:128]
            sb32[:, 2 * m + 1, :] = packed[:, 128:256]
            mine = up[16 * m : 16 * m + 16]
            wide = jnp.concatenate(
                [jnp.where(lane4 == d, mine, 0.0).astype(BF) for d in range(4)] + [zeros], axis=0
            )
            sb32[:, 4 + m, :] = jnp.transpose(nt(wide, rep_up))
        sb2[...] = sb32[...].astype(BF)
        exchange_start(sb2, rb2, 1)
        kvl[...] = (2.0 * nn(low_t, up2[...])).astype(BF)
        igl[...] = nn(back_t, d2t[...]).astype(BF)

    def gradients():
        exchange_wait(sb2, rb2, 1)
        rb32[...] = rb2[...].astype(F32)
        down0, up0 = arrived(0)
        down1, up1 = arrived(1)
        gd_ref[...] = nt(down0, onehot[0]) + nt(down1, onehot[1])
        gu_ref[...] = nt(up0, onehot[0]) + nt(up1, onehot[1])

    for i in range(1, XN):
        ax_copy(i).start()
    for d in range(2):
        b_copy(d, 0).start()
        a_copy(d, 0, x).start()
    spread(0, 0)
    exchange_start(sb1, rb1, 0)
    acc[...] = jnp.zeros_like(acc)
    for i in range(1, XN):
        xs = xmod(x + i)
        ax_wait(xs)
        for d in range(2):
            a_copy(d, 0, xs).start()
    forward_x(0, 0)
    complete_x(0, 0)

    @pl.loop(1, 8)
    def _(k):
        for d in range(2):
            for i in range(XN):
                xs = xmod(x + i)
                a_wait(d, k, xs)

                @pl.when((k < 7) | (lax.div(xs, 2) == d))
                def _():
                    a_copy(d, k, xs).start()

            b_wait(d, k)

            @pl.when(k < 7)
            def _():
                b_copy(d, k).start()

            @pl.when(k == 7)
            def _():
                b_half_copy(d).start()

            spread(d, k)

        @pl.when(k >= 2)
        def _():
            for d in range(2):
                forward_x(d, k - 1)

        @pl.when(k >= 3)
        def _():
            for d in range(2):
                complete_x(d, k - 2)
            block(k - 2)

        @pl.when(k == ADAPT_AT)
        def _():
            adapters()

        @pl.when(k == TILES_AT)
        def _():
            tiles()

    for d in range(2):
        for h in range(2):
            a_wait(d, 8, 2 * d + h)
        b_half_wait(d)
    spread(0, 8)
    for d in range(2):
        forward_x(d, 7)
    for d in range(2):
        complete_x(d, 6)
    block(6)
    forward_x(0, 8)
    for d in range(2):
        complete_x(d, 7)
    block(7)
    gradients()
    complete_x(0, 8)
    block(8)
    ig_ref[...] = (acc[...] + igl[...].astype(F32)).astype(BF)

    total = own_kv[...]
    for t in range(1, TN):
        q = lax.rem(tp + t, TN)
        remote(
            rs_send.at[q], rs_recv.at[q], s_rs.at[q], r_rs.at[q], tp_device(q)
        ).wait_recv()
        total = total + rs_recv[q].astype(F32)
    kv_ref[...] = (total + kvl[...].astype(F32)).astype(BF)

    exchange_drain(sb1, rb1, 0)
    exchange_drain(sb2, rb2, 1)
    for i in range(1, XN):
        ax_copy(i).wait_send()

    @pl.loop(1, TN)
    def _(t):
        ar_copy(t).wait_send()
        rs_copy(lax.rem(tp + t, TN)).wait_send()

    for d in range(2):

        @pl.loop(0, 7)
        def _(k):
            for xs in range(XN):
                a_copy(d, k, xs).wait_send()
            b_copy(d, k).wait_send()

        for h in range(2):
            a_copy(d, 7, 2 * d + h).wait_send()
        b_half_copy(d).wait_send()
    for side in range(2):

        @pl.loop(0, 9)
        def _(k):
            bx_copy(side, 0, k).wait_send()
            bf_copy(side, 0, k).wait_send()

        @pl.loop(1, 8)
        def _(k):
            bx_copy(side, 1, k).wait_send()
            bf_copy(side, 1, k).wait_send()


def fused(tok, wt, cot, idx, dn, up):
    dma = pltpu.SemaphoreType.DMA
    vmem = pl.BlockSpec(memory_space=pltpu.VMEM)
    return pl.pallas_call(
        kernel,
        out_shape=(
            jax.ShapeDtypeStruct((256, 256), BF),
            jax.ShapeDtypeStruct((256, 1024), BF),
            jax.ShapeDtypeStruct((256, 512), F32),
            jax.ShapeDtypeStruct((64, 512), F32),
        ),
        in_specs=[vmem] * 6,
        out_specs=[vmem] * 4,
        scratch_shapes=[
            pltpu.VMEM((2048, LA), BF),
            pltpu.VMEM((2048, LB), BF),
            pltpu.VMEM((256, 1024), F32),
            pltpu.VMEM((256, 256), F32),
            pltpu.VMEM((TN, 256, 256), BF),
            pltpu.VMEM((TN, 256, 256), BF),
            pltpu.VMEM((256, 256), BF),
            pltpu.VMEM((256, 1024), BF),
            pltpu.VMEM((2, 512, FN), BF),
            pltpu.VMEM((FN, 8, 128), F32),
            pltpu.VMEM((FN, 8, 128), BF),
            pltpu.VMEM((FN, 8, 128), BF),
            pltpu.VMEM((FN, 8, 128), F32),
            pltpu.VMEM((FN, 8, 128), BF),
            pltpu.VMEM((FN, 8, 128), BF),
            pltpu.VMEM((32, 1024), BF),
            pltpu.VMEM((32, 256), BF),
            pltpu.VMEM((32, 256), F32),
            pltpu.VMEM((TN, 32, 256), F32),
            dma((2,)),
            dma((2, 8, XN)),
            dma((2, 9, XN)),
            dma((XN,)),
            dma((XN,)),
            dma((2, 8)),
            dma((2, 9)),
            dma((2, 16)),
            dma((2, 16)),
            dma((2, 16)),
            dma((2, 16)),
            dma((TN,)),
            dma((TN,)),
            dma((TN,)),
            dma((TN,)),
            dma((2,)),
            dma((2,)),
            dma((2,)),
        ],
        compiler_params=pltpu.CompilerParams(
            collective_id=0, has_side_effects=True, vmem_limit_bytes=56 << 20
        ),
    )(tok, wt, cot, idx, dn, up)


def local(tokens, frozen_weight, cotangent, block_adapter_index, down_weight, up_weight):
    tok = tokens.reshape(256, 1024)
    cot = cotangent.reshape(256, 2048)
    wt = frozen_weight.T
    dn = down_weight.transpose(1, 2, 0).reshape(256, 512)
    up = up_weight.transpose(2, 1, 0).reshape(64, 512)
    kv, ig, gd, gu = fused(tok, wt, cot, block_adapter_index, dn, up)
    return (
        kv.reshape(2, 128, 256),
        ig.reshape(2, 128, 1024),
        gd.reshape(16, 16, 512).transpose(2, 0, 1),
        gu.reshape(4, 16, 512).transpose(2, 1, 0),
    )


def solution(mesh):
    finer = Mesh(mesh.devices.reshape(ZN, XN, 4, 2), ("z", "x", "y", "c"))
    return jax.shard_map(
        local,
        mesh=finer,
        in_specs=(
            P(None, PLANE, TP),
            P(TP, PLANE),
            P(None, PLANE, None),
            P(),
            P(None, ALL, None),
            P(None, None, ALL),
        ),
        out_specs=(
            P(None, PLANE, TP),
            P(None, PLANE, TP),
            P(None, ALL, None),
            P(None, None, ALL),
        ),
        check_vma=False,
    )
```

time: 203 us -> 89.5 us (0.44)
  the two profiles are of different devices: /device:TPU:1 before, /device:TPU:81 now
where the time goes in v1:
time: 89.5 us; the launch traced here: 89.2 us
  Pallas kernels  81.7 us (91%)
  local copies, waits for them, and re-layouts  6.78 us (8%)
    pallas_call x1, Pallas kernels, fused(): pl.pallas_call(kernel, out_shape=(jax.ShapeDtypeStruct((256, 256), BF), j...  81.7 us
    unnamed x7, local copies, waits for them, and re-layouts  3.59 us

profile of v1, /device:TPU:81, one launch (start us, length us, event | category | flops | bytes accessed | tf_op | source)
XLA Modules:
  0.0 89.2 jit_solution(14408335808771407149)
XLA Ops:
  0.6 1.5 %copy.10 = bf16[4,16,512]{2,1,0:T(8,128)(2,1)} copy(bf16[4,16,512]{2,0,1:T(4,128)(2,1)} %bitcast.27) | data formatting | bytes 131072 | tf_op jit(solution)/shard_map/transpose | solution.py:520
  2.1 81.7 %shard_map.93 = (bf16[256,256]{1,0:T(8,128)(2,1)}, bf16[256,1024]{1,0:T(8,128)(2,1)}, f32[256,512]{1,0:T(8,128)}, f32[64,512]{1,0:T(8,128)}) custom-call(bf16[256,1024]{1,0:T(8,128)(2,1)} %bitcast.18, bf16[32,1024]{1,0:T(8,128)(2,1)} %bitcast.26, bf16[256,2048]{1,0:T(8,128)(2,1)} %bitcast.17, s32[2,64]{1,0:T(2,128)} %idx_ref.1, bf16[256,512]{1,0:T(8,128)(2,1)} %bitcast.21, ...), custom_call_target="tpu_custom_call" | custom-call | tf_op jit(solution)/shard_map/pallas_call | solution.py:460
  83.9 0.0 copy-start.1
  83.9 1.7 %copy.13 = f32[4,16,512]{2,0,1:T(4,128)} copy(f32[4,16,512]{2,1,0:T(8,128)} %bitcast.25) | data formatting | bytes 262144 | tf_op jit(solution)/shard_map/reshape | solution.py:526
  85.6 1.6 %copy.17 = bf16[2,128,256]{2,1,0:T(8,128)(2,1)} copy(bf16[2,128,256]{2,1,0:T(8,128)(2,1)} %bitcast.24) | data formatting | bytes 262144
  87.1 0.0 copy-done.1
  87.1 0.0 copy-start
  87.2 0.8 copy.18
  87.9 0.4 copy-done
  88.4 0.8 copy.19
Async XLA Ops:
  83.9 3.3 %copy-start.1 = (bf16[256,1024]{1,0:T(8,128)(2,1)S(1)}, bf16[256,1024]{1,0:T(8,128)(2,1)}, u32[]{:S(2)}) copy-start(bf16[256,1024]{1,0:T(8,128)(2,1)} %get-tuple-element.9) | copy-start | bytes 1572868
  87.1 1.2 %copy-start = (f32[256,512]{1,0:T(8,128)S(1)}, f32[256,512]{1,0:T(8,128)}, u32[]{:S(2)}) copy-start(f32[256,512]{1,0:T(8,128)} %get-tuple-element.10) | copy-start | bytes 1572868

commit v2 on v1

--- a/solution.py
+++ b/solution.py
@@ -20,8 +20,8 @@
 NA = 2
 LA = NA * 128
 LB = 1024 - LA
-ADAPT_AT = 3
-TILES_AT = 5
+ADAPT_AT = 4
+TILES_AT = 6
 
 
 def nt(a, b):
@@ -36,12 +36,34 @@
     return lax.broadcasted_iota(jnp.int32, shape, dim)
 
 
+def arrived(ref, m):
+    down = [jnp.transpose(ref[:, 2 * m + h, :]) for h in range(2)]
+    up = jnp.transpose(ref[:, 4 + m, :])[0:64, :]
+    return jnp.concatenate(down, axis=0).astype(BF), up.astype(BF)
+
+
+def finish(kv_in, ig_in, got_in, idx_ref, kv_ref, ig_ref, gd_ref, gu_ref, wide):
+    kv_ref[...] = kv_in[...]
+    ig_ref[...] = ig_in[...]
+    wide[...] = got_in[...].astype(F32)
+    downs, ups = [], []
+    for m in range(2):
+        pick = jnp.where(iota((512, FN), 0) == idx_ref[m : m + 1, :], 1.0, 0.0).astype(BF)
+        down, up = arrived(wide, m)
+        downs.append(nt(down, pick))
+        ups.append(nt(up, pick))
+    gd_ref[...] = downs[0] + downs[1]
+    total = ups[0] + ups[1]
+    for c in range(4):
+        gu_ref[:, c, :] = total[16 * c : 16 * c + 16]
+
+
 def kernel(
-    tok_ref, wt_ref, cot_ref, idx_ref, dn_ref, up_ref,
-    kv_ref, ig_ref, gd_ref, gu_ref,
+    tok_in, wt_in, cot_in, idx_in, dn_in, up_in,
+    kv_ref, ig_ref, got_ref, ids_ref,
     wa, wb, acc, own_kv, rs_send, rs_recv, kvl, igl,
-    onehot, sb32, sb1, sb2, rb32, rb1, rb2, d2t, up2, ar_send, ar_recv,
-    s_loc, s_a, r_a, s_ax, r_ax, s_b, r_b, s_bx, r_bx, s_bf, r_bf,
+    tok_ref, cot_ref, idx_ref, dn_ref, up_ref, up32, sb32, sb1, sb2, rb32, rb1, rb2, d2t, up2, ar_send, ar_recv,
+    wave, s_b8, r_b8, s_loc, s_a, r_a, s_ax, r_ax, s_b, r_b, s_bx, r_bx, s_bf, r_bf,
     s_rs, r_rs, s_ar, r_ar, s_e, r_e, l_e,
 ):
     z, x = lax.axis_index("z"), lax.axis_index("x")
@@ -70,46 +92,59 @@
         return pl.ds(pl.multiple_of(base, size), size)
 
     barrier = pltpu.get_barrier_semaphore()
-
-    @pl.loop(1, FN)
-    def _(p):
+    near = [{"z": zmod(z + 1)}, {"z": zmod(z - 1)}]
+    near += [{"x": xmod(x + i)} for i in range(1, XN)]
+    near += [tp_device(lax.rem(tp + t, TN)) for t in range(1, TN)]
+    for device in near:
+        pl.semaphore_signal(barrier, 1, device_id=device, device_id_type=MESH)
+
+    own_rows = rows_at(f * 32, 32)
+    loads = [
+        pltpu.make_async_copy(src, dst, s_loc.at[n])
+        for n, (src, dst) in enumerate(
+            (
+                (wt_in.at[:, 0:LA], wa.at[own_rows]),
+                (wt_in.at[:, LA:1024], wb.at[own_rows]),
+                (idx_in, idx_ref),
+                (up_in, up_ref),
+                (dn_in, dn_ref),
+                (tok_in, tok_ref),
+                (cot_in, cot_ref),
+            )
+        )
+    ]
+    for load in loads:
+        load.start()
+    loads[0].wait()
+    loads[1].wait()
+    pl.semaphore_wait(barrier, len(near))
+
+    def wave_on(d, k):
         pl.semaphore_signal(
-            barrier, 1, device_id=plane_device(lax.rem(f + p, FN)), device_id_type=MESH
+            wave.at[d, k], 1, device_id=ring_device(d), device_id_type=MESH
         )
 
-    @pl.loop(1, TN)
-    def _(t):
-        pl.semaphore_signal(
-            barrier, 1, device_id=tp_device(lax.rem(tp + t, TN)), device_id_type=MESH
-        )
-
-    own_rows = rows_at(f * 32, 32)
-    own_a = pltpu.make_async_copy(wt_ref.at[:, 0:LA], wa.at[own_rows], s_loc.at[0])
-    own_b = pltpu.make_async_copy(wt_ref.at[:, LA:1024], wb.at[own_rows], s_loc.at[1])
-    own_a.start()
-    own_b.start()
-
-    zeros_up = jnp.zeros((64, FN), F32)
-    sb32[...] = jnp.zeros_like(sb32)
-    for m in range(2):
+    def wave_step(k):
+        for d in range(2):
+            if k < 8 or d == 0:
+                pl.semaphore_wait(wave.at[d, k], 1)
+            if k < 7 or (k == 7 and d == 0):
+                wave_on(d, k + 1)
+
+    def select(m):
         pick = jnp.where(iota((512, FN), 0) == idx_ref[m : m + 1, :], 1.0, 0.0).astype(BF)
-        onehot[m] = pick
         down = jnp.transpose(nn(dn_ref[...], pick))
         sb32[:, 2 * m, :] = down[:, 0:128]
         sb32[:, 2 * m + 1, :] = down[:, 128:256]
-        up = jnp.concatenate([nn(up_ref[...], pick), zeros_up], axis=0)
+        wide = jnp.concatenate([up32[:, c, :] for c in range(4)], axis=0).astype(BF)
+        up = jnp.concatenate([nn(wide, pick), jnp.zeros((64, FN), F32)], axis=0)
         sb32[:, 4 + m, :] = jnp.transpose(up)
-    sb1[...] = sb32[...].astype(BF)
-
-    own_a.wait()
-    own_b.wait()
-    pl.semaphore_wait(barrier, FN - 1 + TN - 1)
 
     def exchange_start(src, dst, n):
         own = pltpu.make_async_copy(src.at[f], dst.at[f], l_e.at[n])
         own.start()
 
-        @pl.loop(1, FN)
+        @pl.loop(1, FN, unroll=7)
         def _(p):
             q = lax.rem(f + p, FN)
             remote(src.at[q], dst.at[f], s_e.at[n], r_e.at[n], plane_device(q)).start()
@@ -204,6 +239,16 @@
         rows = bf_rows(side, d, k, xmod(x + 2))
         remote(rows, rows, s_bf.at[side, n], r_bf.at[side, n], x_device(side)).wait_recv()
 
+    def b8_copy(d, i):
+        rows = b_half(d, 8)
+        return remote(rows, rows, s_b8.at[d, i], r_b8.at[d, x], {"x": xmod(x + i)})
+
+    def b8_wait(d, i):
+        from_x = xmod(x + i)
+        zz = zmod(z + 8)
+        rows = wb.at[rows_at(zz * 128 + from_x * 32 + 16 * d, 16)]
+        remote(rows, rows, s_b8.at[d, i], r_b8.at[d, from_x], {"x": from_x}).wait_recv()
+
     def spread(d, k):
         for side in range(2):
             bx_copy(side, d, k).start()
@@ -222,26 +267,37 @@
             rs_send.at[c], rs_recv.at[tp], s_rs.at[c], r_rs.at[tp], tp_device(c)
         )
 
-    def block(k):
+    def piece(k, j):
         odd = lax.rem(z + k, 2)
         start = zmod(jnp.where(odd == 1, z + k - 1, z - k))
         c = lax.div(start, 2)
-        rows = rows_at(c * 256, 256)
-        w_a, w_b = wa[rows, :], wb[rows, :]
-        part = nt(tok_ref[:, 0:LA], w_a) + nt(tok_ref[:, LA:1024], w_b)
-
-        @pl.when(c == tp)
-        def _():
-            own_kv[...] = part
-
-        @pl.when(c != tp)
-        def _():
-            rs_send[c] = part.astype(BF)
-            rs_copy(c).start()
-
-        cot = cot_ref[:, rows]
-        acc[:, 0:LA] += nn(cot, w_a)
-        acc[:, LA:1024] += nn(cot, w_b)
+        if j < 2:
+            rows = rows_at(c * 256 + 128 * j, 128)
+            cols = slice(128 * j, 128 * j + 128)
+            part = nt(tok_ref[:, 0:LA], wa[rows, :]) + nt(tok_ref[:, LA:1024], wb[rows, :])
+
+            @pl.when(c == tp)
+            def _():
+                own_kv[:, cols] = part
+
+            @pl.when(c != tp)
+            def _():
+                rs_send[c, :, cols] = part.astype(BF)
+                if j == 1:
+                    rs_copy(c).start()
+
+        else:
+            rows = rows_at(c * 256, 256)
+            cot = cot_ref[:, rows]
+            if j == 2:
+                acc[:, 0:LA] += nn(cot, wa[rows, :])
+                acc[:, LA:512] += nn(cot, wb[rows, 0 : 512 - LA])
+            else:
+                acc[:, 512:1024] += nn(cot, wb[rows, 512 - LA : LB])
+
+    def block(k):
+        for j in range(4):
+            piece(k, j)
 
     rep = jnp.where(lax.div(iota((FN, 1024), 1), 16) == iota((FN, 1024), 0), 1.0, 0.0).astype(BF)
     rep_up = jnp.where(lax.div(iota((FN, 256), 1), 4) == iota((FN, 256), 0), 1.0, 0.0).astype(BF)
@@ -250,13 +306,6 @@
     first = iota((16, 256), 1) < 128
     cot_cols = pl.ds(pl.multiple_of(tp * 256, 256), 256)
 
-    def arrived(m):
-        down = jnp.concatenate(
-            [jnp.transpose(rb32[:, 2 * m, :]), jnp.transpose(rb32[:, 2 * m + 1, :])], axis=0
-        )
-        up = jnp.transpose(rb32[:, 4 + m, :])[0:64, :]
-        return down.astype(BF), up.astype(BF)
-
     def folded(value):
         return jnp.where(first, value[0:16], value[16:32])
 
@@ -269,7 +318,7 @@
         exchange_wait(sb1, rb1, 0)
         rb32[...] = rb1[...].astype(F32)
         for m in range(2):
-            down, up = arrived(m)
+            down, up = arrived(rb32, m)
             wide = nn(down, rep)
             total = jnp.zeros((16, 1024), F32)
             for d in range(16):
@@ -326,63 +375,86 @@
         kvl[...] = (2.0 * nn(low_t, up2[...])).astype(BF)
         igl[...] = nn(back_t, d2t[...]).astype(BF)
 
-    def gradients():
-        exchange_wait(sb2, rb2, 1)
-        rb32[...] = rb2[...].astype(F32)
-        down0, up0 = arrived(0)
-        down1, up1 = arrived(1)
-        gd_ref[...] = nt(down0, onehot[0]) + nt(down1, onehot[1])
-        gu_ref[...] = nt(up0, onehot[0]) + nt(up1, onehot[1])
-
     for i in range(1, XN):
         ax_copy(i).start()
     for d in range(2):
         b_copy(d, 0).start()
         a_copy(d, 0, x).start()
+        wave_on(d, 1)
     spread(0, 0)
-    exchange_start(sb1, rb1, 0)
-    acc[...] = jnp.zeros_like(acc)
+    for load in loads[2:5]:
+        load.wait()
+    up32[...] = up_ref[...].astype(F32)
+    sb32[...] = jnp.zeros_like(sb32)
+
+    def ring_b(k):
+        for d in range(2):
+            b_wait(d, k)
+
+            @pl.when(k < 7)
+            def _():
+                b_copy(d, k).start()
+
+            @pl.when(k == 7)
+            def _():
+                b_half_copy(d).start()
+
+            spread(d, k)
+
+    def ring_a(k, i):
+        xs = xmod(x + i)
+        for d in range(2):
+            a_wait(d, k, xs)
+
+            @pl.when((k < 7) | (lax.div(xs, 2) == d))
+            def _():
+                a_copy(d, k, xs).start()
+
+    wave_step(1)
+    select(0)
+    wave_step(2)
     for i in range(1, XN):
         xs = xmod(x + i)
         ax_wait(xs)
         for d in range(2):
             a_copy(d, 0, xs).start()
+    select(1)
+    wave_step(3)
+    sb1[...] = sb32[...].astype(BF)
+    ring_b(1)
+    wave_step(4)
+    for i in range(XN):
+        ring_a(1, i)
+    wave_step(5)
     forward_x(0, 0)
-    complete_x(0, 0)
-
-    @pl.loop(1, 8)
+    for k in range(6, 9):
+        wave_step(k)
+    exchange_start(sb1, rb1, 0)
+    acc[...] = jnp.zeros_like(acc)
+    loads[5].wait()
+    loads[6].wait()
+
+    @pl.loop(2, 8)
     def _(k):
+        ring_b(k)
+        for i in range(XN):
+            ring_a(k, i)
+
+            @pl.when(k >= 4)
+            def _():
+                piece(k - 3, i)
+
         for d in range(2):
-            for i in range(XN):
-                xs = xmod(x + i)
-                a_wait(d, k, xs)
-
-                @pl.when((k < 7) | (lax.div(xs, 2) == d))
-                def _():
-                    a_copy(d, k, xs).start()
-
-            b_wait(d, k)
-
-            @pl.when(k < 7)
-            def _():
-                b_copy(d, k).start()
-
-            @pl.when(k == 7)
-            def _():
-                b_half_copy(d).start()
-
-            spread(d, k)
-
-        @pl.when(k >= 2)
+            forward_x(d, k - 1)
+
+        @pl.when(k == 2)
         def _():
-            for d in range(2):
-                forward_x(d, k - 1)
+            complete_x(0, 0)
 
         @pl.when(k >= 3)
         def _():
             for d in range(2):
                 complete_x(d, k - 2)
-            block(k - 2)
 
         @pl.when(k == ADAPT_AT)
         def _():
@@ -393,23 +465,31 @@
             tiles()
 
     for d in range(2):
-        for h in range(2):
+        b_half_wait(d)
+        for i in range(1, XN):
+            b8_copy(d, i).start()
+    for h in range(2):
+        for d in range(2):
             a_wait(d, 8, 2 * d + h)
-        b_half_wait(d)
-    spread(0, 8)
+        piece(5, h)
     for d in range(2):
         forward_x(d, 7)
+    piece(5, 2)
+    piece(5, 3)
     for d in range(2):
         complete_x(d, 6)
     block(6)
-    forward_x(0, 8)
     for d in range(2):
         complete_x(d, 7)
     block(7)
-    gradients()
-    complete_x(0, 8)
+    for d in range(2):
+        for i in range(1, XN):
+            b8_wait(d, i)
     block(8)
     ig_ref[...] = (acc[...] + igl[...].astype(F32)).astype(BF)
+    exchange_wait(sb2, rb2, 1)
+    got_ref[...] = rb2[...]
+    ids_ref[...] = idx_ref[...]
 
     total = own_kv[...]
     for t in range(1, TN):
@@ -441,9 +521,12 @@
         for h in range(2):
             a_copy(d, 7, 2 * d + h).wait_send()
         b_half_copy(d).wait_send()
+    for d in range(2):
+        for i in range(1, XN):
+            b8_copy(d, i).wait_send()
     for side in range(2):
 
-        @pl.loop(0, 9)
+        @pl.loop(0, 8)
         def _(k):
             bx_copy(side, 0, k).wait_send()
             bf_copy(side, 0, k).wait_send()
@@ -457,15 +540,15 @@
 def fused(tok, wt, cot, idx, dn, up):
     dma = pltpu.SemaphoreType.DMA
     vmem = pl.BlockSpec(memory_space=pltpu.VMEM)
-    return pl.pallas_call(
+    kv, ig, got, ids = pl.pallas_call(
         kernel,
         out_shape=(
             jax.ShapeDtypeStruct((256, 256), BF),
             jax.ShapeDtypeStruct((256, 1024), BF),
-            jax.ShapeDtypeStruct((256, 512), F32),
-            jax.ShapeDtypeStruct((64, 512), F32),
+            jax.ShapeDtypeStruct((FN, 8, 128), BF),
+            jax.ShapeDtypeStruct((2, FN), jnp.int32),
         ),
-        in_specs=[vmem] * 6,
+        in_specs=[pl.BlockSpec(memory_space=pltpu.HBM)] * 6,
         out_specs=[vmem] * 4,
         scratch_shapes=[
             pltpu.VMEM((2048, LA), BF),
@@ -476,7 +559,12 @@
             pltpu.VMEM((TN, 256, 256), BF),
             pltpu.VMEM((256, 256), BF),
             pltpu.VMEM((256, 1024), BF),
-            pltpu.VMEM((2, 512, FN), BF),
+            pltpu.VMEM((256, 1024), BF),
+            pltpu.VMEM((256, 2048), BF),
+            pltpu.VMEM((2, FN), jnp.int32),
+            pltpu.VMEM((256, 512), BF),
+            pltpu.VMEM((16, 4, 512), BF),
+            pltpu.VMEM((16, 4, 512), F32),
             pltpu.VMEM((FN, 8, 128), F32),
             pltpu.VMEM((FN, 8, 128), BF),
             pltpu.VMEM((FN, 8, 128), BF),
@@ -487,7 +575,10 @@
             pltpu.VMEM((32, 256), BF),
             pltpu.VMEM((32, 256), F32),
             pltpu.VMEM((TN, 32, 256), F32),
-            dma((2,)),
+            pltpu.SemaphoreType.REGULAR((2, 9)),
+            dma((2, XN)),
+            dma((2, XN)),
+            dma((7,)),
             dma((2, 8, XN)),
             dma((2, 9, XN)),
             dma((XN,)),
@@ -507,9 +598,22 @@
             dma((2,)),
         ],
         compiler_params=pltpu.CompilerParams(
-            collective_id=0, has_side_effects=True, vmem_limit_bytes=56 << 20
+            collective_id=0, has_side_effects=True, vmem_limit_bytes=32 << 20
         ),
-    )(tok, wt, cot, idx, dn, up)
+    )(*(pltpu.with_memory_space_constraint(v, pltpu.HBM) for v in (tok, wt, cot, idx, dn, up)))
+    return pl.pallas_call(
+        finish,
+        out_shape=(
+            jax.ShapeDtypeStruct((256, 256), BF),
+            jax.ShapeDtypeStruct((256, 1024), BF),
+            jax.ShapeDtypeStruct((256, 512), F32),
+            jax.ShapeDtypeStruct((16, 4, 512), F32),
+        ),
+        in_specs=[vmem] * 4,
+        out_specs=[vmem] * 4,
+        scratch_shapes=[pltpu.VMEM((FN, 8, 128), F32)],
+        compiler_params=pltpu.CompilerParams(vmem_limit_bytes=16 << 20),
+    )(kv, ig, got, ids)
 
 
 def local(tokens, frozen_weight, cotangent, block_adapter_index, down_weight, up_weight):
@@ -517,13 +621,13 @@
     cot = cotangent.reshape(256, 2048)
     wt = frozen_weight.T
     dn = down_weight.transpose(1, 2, 0).reshape(256, 512)
-    up = up_weight.transpose(2, 1, 0).reshape(64, 512)
+    up = up_weight.transpose(1, 2, 0)
     kv, ig, gd, gu = fused(tok, wt, cot, block_adapter_index, dn, up)
     return (
         kv.reshape(2, 128, 256),
         ig.reshape(2, 128, 1024),
         gd.reshape(16, 16, 512).transpose(2, 0, 1),
-        gu.reshape(4, 16, 512).transpose(2, 1, 0),
+        gu.transpose(2, 0, 1),
     )
 
 

time: 89.5 us -> 76.7 us (0.86)
  the two profiles are of different devices: /device:TPU:81 before, /device:TPU:16 now
where the time goes in v2:
time: 76.7 us; the launch traced here: 76.5 us
  Pallas kernels  75.9 us (99%)
    pallas_call x1, Pallas kernels, fused(): pl.pallas_call(kernel, out_shape=(jax.ShapeDtypeStruct((256, 256), BF), j...  74.4 us

profile of v2, /device:TPU:16, one launch (start us, length us, event | category | flops | bytes accessed | tf_op | source)
XLA Modules:
  0.0 76.5 jit_solution(5111608201810723592)
XLA Ops:
  0.6 74.4 %shard_map.93 = (bf16[256,256]{1,0:T(8,128)(2,1)S(1)}, bf16[256,1024]{1,0:T(8,128)(2,1)S(1)}, bf16[64,8,128]{2,1,0:T(8,128)(2,1)S(1)}, s32[2,64]{1,0:T(2,128)S(1)}) custom-call(bf16[256,1024]{1,0:T(8,128)(2,1)} %bitcast.14, bf16[32,1024]{1,0:T(8,128)(2,1)} %bitcast.16, bf16[256,2048]{1,0:T(8,128)(2,1)} %bitcast.13, s32[2,64]{1,0:T(2,128)} %idx_in.1, ...), custom_call_target="tpu_custom_call" | custom-call | tf_op jit(solution)/shard_map/pallas_call | solution.py:543
  75.1 1.5 %shard_map.94 = (bf16[256,256]{1,0:T(8,128)(2,1)}, bf16[256,1024]{1,0:T(8,128)(2,1)}, f32[256,512]{1,0:T(8,128)}, f32[16,4,512]{2,1,0:T(4,128)}) custom-call(bf16[256,256]{1,0:T(8,128)(2,1)S(1)} %get-tuple-element.12.kv_in, bf16[256,1024]{1,0:T(8,128)(2,1)S(1)} %get-tuple-element.13.ig_in, bf16[64,8,128]{2,1,0:T(8,128)(2,1)S(1)} %get-tuple-element.14.got_in, ...), custom_call_target="tpu_custom_call" | custom-call | tf_op jit(solution)/shard_map/pallas_call | solution.py:604

commit v3 on v2

--- a/solution.py
+++ b/solution.py
@@ -20,8 +20,8 @@
 NA = 2
 LA = NA * 128
 LB = 1024 - LA
-ADAPT_AT = 4
-TILES_AT = 6
+ADAPT_AT = 5
+TILES_AT = 7
 
 
 def nt(a, b):
@@ -61,7 +61,7 @@
 def kernel(
     tok_in, wt_in, cot_in, idx_in, dn_in, up_in,
     kv_ref, ig_ref, got_ref, ids_ref,
-    wa, wb, acc, own_kv, rs_send, rs_recv, kvl, igl,
+    wa, wb, acc, own_kv, rs_send, rs_recv, low_t, back_t,
     tok_ref, cot_ref, idx_ref, dn_ref, up_ref, up32, sb32, sb1, sb2, rb32, rb1, rb2, d2t, up2, ar_send, ar_recv,
     wave, s_b8, r_b8, s_loc, s_a, r_a, s_ax, r_ax, s_b, r_b, s_bx, r_bx, s_bf, r_bf,
     s_rs, r_rs, s_ar, r_ar, s_e, r_e, l_e,
@@ -172,27 +172,27 @@
 
     def a_copy(d, k, xs):
         rows = wa.at[a_rows(d, k, xs)]
-        return remote(rows, rows, s_a.at[d, k, xs], r_a.at[d, k + 1, xs], ring_device(d))
+        return remote(rows, rows, s_a.at[d], r_a.at[d, k + 1, xs], ring_device(d))
 
     def a_wait(d, k, xs):
         rows = wa.at[a_rows(d, k, xs)]
-        remote(rows, rows, s_a.at[d, 0, xs], r_a.at[d, k, xs], ring_device(d)).wait_recv()
+        remote(rows, rows, s_a.at[d], r_a.at[d, k, xs], ring_device(d)).wait_recv()
 
     def ax_copy(i):
         rows = wa.at[own_rows]
-        return remote(rows, rows, s_ax.at[i], r_ax.at[x], {"x": xmod(x + i)})
+        return remote(rows, rows, s_ax, r_ax.at[x], {"x": xmod(x + i)})
 
     def ax_wait(xs):
         rows = wa.at[a_rows(0, 0, xs)]
-        remote(rows, rows, s_ax.at[1], r_ax.at[xs], {"x": xmod(x + 1)}).wait_recv()
+        remote(rows, rows, s_ax, r_ax.at[xs], {"x": xmod(x + 1)}).wait_recv()
 
     def b_copy(d, k):
         rows = wb.at[b_rows(d, k)]
-        return remote(rows, rows, s_b.at[d, k], r_b.at[d, k + 1], ring_device(d))
+        return remote(rows, rows, s_b.at[d], r_b.at[d, k + 1], ring_device(d))
 
     def b_wait(d, k):
         rows = wb.at[b_rows(d, k)]
-        remote(rows, rows, s_b.at[d, 0], r_b.at[d, k], ring_device(d)).wait_recv()
+        remote(rows, rows, s_b.at[d], r_b.at[d, k], ring_device(d)).wait_recv()
 
     def b_half(d, k):
         zz = zmod(z - k) if d == 0 else zmod(z + k)
@@ -200,11 +200,11 @@
 
     def b_half_copy(d):
         rows = b_half(d, 7)
-        return remote(rows, rows, s_b.at[d, 7], r_b.at[d, 8], ring_device(d))
+        return remote(rows, rows, s_b.at[d], r_b.at[d, 8], ring_device(d))
 
     def b_half_wait(d):
         rows = b_half(d, 8)
-        remote(rows, rows, s_b.at[d, 7], r_b.at[d, 8], ring_device(d)).wait_recv()
+        remote(rows, rows, s_b.at[d], r_b.at[d, 8], ring_device(d)).wait_recv()
 
     def slot(d, k):
         return k if d == 0 else 8 + k
@@ -218,12 +218,12 @@
     def bx_copy(side, d, k):
         rows = bx_rows(d, k, x)
         n = slot(d, k)
-        return remote(rows, rows, s_bx.at[side, n], r_bx.at[side, n], x_device(side))
+        return remote(rows, rows, s_bx.at[side], r_bx.at[side, n], x_device(side))
 
     def bx_wait(side, d, k):
         n = slot(d, k)
         rows = bx_rows(d, k, xmod(x - 1) if side == 0 else xmod(x + 1))
-        remote(rows, rows, s_bx.at[side, n], r_bx.at[side, n], x_device(side)).wait_recv()
+        remote(rows, rows, s_bx.at[side], r_bx.at[side, n], x_device(side)).wait_recv()
 
     def bf_rows(side, d, k, from_x):
         zz = zmod(z - k) if d == 0 else zmod(z + k)
@@ -232,22 +232,22 @@
     def bf_copy(side, d, k):
         n = slot(d, k)
         rows = bf_rows(side, d, k, xmod(x - 1) if side == 0 else xmod(x + 1))
-        return remote(rows, rows, s_bf.at[side, n], r_bf.at[side, n], x_device(side))
+        return remote(rows, rows, s_bf.at[side], r_bf.at[side, n], x_device(side))
 
     def bf_wait(side, d, k):
         n = slot(d, k)
         rows = bf_rows(side, d, k, xmod(x + 2))
-        remote(rows, rows, s_bf.at[side, n], r_bf.at[side, n], x_device(side)).wait_recv()
+        remote(rows, rows, s_bf.at[side], r_bf.at[side, n], x_device(side)).wait_recv()
 
     def b8_copy(d, i):
         rows = b_half(d, 8)
-        return remote(rows, rows, s_b8.at[d, i], r_b8.at[d, x], {"x": xmod(x + i)})
+        return remote(rows, rows, s_b8, r_b8.at[d, x], {"x": xmod(x + i)})
 
     def b8_wait(d, i):
         from_x = xmod(x + i)
         zz = zmod(z + 8)
         rows = wb.at[rows_at(zz * 128 + from_x * 32 + 16 * d, 16)]
-        remote(rows, rows, s_b8.at[d, i], r_b8.at[d, from_x], {"x": from_x}).wait_recv()
+        remote(rows, rows, s_b8, r_b8.at[d, from_x], {"x": from_x}).wait_recv()
 
     def spread(d, k):
         for side in range(2):
@@ -262,38 +262,43 @@
         for side in range(2):
             bf_wait(side, d, k)
 
-    def rs_copy(c):
+    def rs_copy(zz):
+        c, h = lax.div(zz, 2), lax.rem(zz, 2)
         return remote(
-            rs_send.at[c], rs_recv.at[tp], s_rs.at[c], r_rs.at[tp], tp_device(c)
+            rs_send.at[zz], rs_recv.at[tp, h], s_rs, r_rs.at[tp, h], tp_device(c)
         )
 
-    def piece(k, j):
+    def kv_piece(d, k):
+        zz = zmod(z - k) if d == 0 else zmod(z + k)
+        c = lax.div(zz, 2)
+        rows = rows_at(zz * 128, 128)
+        part = nt(tok_ref[:, 0:LA], wa[rows, :]) + nt(tok_ref[:, LA:1024], wb[rows, :])
+
+        @pl.when(c == tp)
+        def _():
+            own_kv[lax.rem(zz, 2)] = part
+
+        @pl.when(c != tp)
+        def _():
+            rs_send[zz] = part.astype(BF)
+            rs_copy(zz).start()
+
+    def ig_piece(k, j):
         odd = lax.rem(z + k, 2)
         start = zmod(jnp.where(odd == 1, z + k - 1, z - k))
-        c = lax.div(start, 2)
+        rows = rows_at(start * 128, 256)
+        cot = cot_ref[:, rows]
+        if j == 0:
+            acc[:, 0:LA] += nn(cot, wa[rows, :])
+            acc[:, LA:512] += nn(cot, wb[rows, 0 : 512 - LA])
+        else:
+            acc[:, 512:1024] += nn(cot, wb[rows, 512 - LA : LB])
+
+    def piece(k, j):
         if j < 2:
-            rows = rows_at(c * 256 + 128 * j, 128)
-            cols = slice(128 * j, 128 * j + 128)
-            part = nt(tok_ref[:, 0:LA], wa[rows, :]) + nt(tok_ref[:, LA:1024], wb[rows, :])
-
-            @pl.when(c == tp)
-            def _():
-                own_kv[:, cols] = part
-
-            @pl.when(c != tp)
-            def _():
-                rs_send[c, :, cols] = part.astype(BF)
-                if j == 1:
-                    rs_copy(c).start()
-
+            kv_piece(j, k)
         else:
-            rows = rows_at(c * 256, 256)
-            cot = cot_ref[:, rows]
-            if j == 2:
-                acc[:, 0:LA] += nn(cot, wa[rows, :])
-                acc[:, LA:512] += nn(cot, wb[rows, 0 : 512 - LA])
-            else:
-                acc[:, 512:1024] += nn(cot, wb[rows, 512 - LA : LB])
+            ig_piece(k, j - 2)
 
     def block(k):
         for j in range(4):
@@ -339,20 +344,21 @@
 
     def ar_copy(t):
         q = lax.rem(tp + t, TN)
-        return remote(ar_send, ar_recv.at[tp], s_ar.at[t], r_ar.at[tp], tp_device(q))
+        return remote(ar_send, ar_recv.at[tp], s_ar, r_ar.at[tp], tp_device(q))
 
     def tiles():
         @pl.loop(1, TN)
         def _(t):
             q = lax.rem(tp + t, TN)
-            remote(ar_send, ar_recv.at[q], s_ar.at[t], r_ar.at[q], tp_device(q)).wait_recv()
+            remote(ar_send, ar_recv.at[q], s_ar, r_ar.at[q], tp_device(q)).wait_recv()
 
         total = ar_recv[0]
         for q in range(1, TN):
             total = total + ar_recv[q]
         low = unfolded(total[0:16].astype(BF).astype(F32))
         back = unfolded(total[16:32].astype(BF).astype(F32))
-        low_t, back_t = jnp.transpose(low).astype(BF), jnp.transpose(back).astype(BF)
+        low_t[...] = jnp.transpose(low).astype(BF)
+        back_t[...] = jnp.transpose(back).astype(BF)
         low, back = low.astype(BF), back.astype(BF)
         down = nn(back, tok_ref[...])
         up = 2.0 * nn(low, cot_ref[:, cot_cols])
@@ -372,8 +378,6 @@
             sb32[:, 4 + m, :] = jnp.transpose(nt(wide, rep_up))
         sb2[...] = sb32[...].astype(BF)
         exchange_start(sb2, rb2, 1)
-        kvl[...] = (2.0 * nn(low_t, up2[...])).astype(BF)
-        igl[...] = nn(back_t, d2t[...]).astype(BF)
 
     for i in range(1, XN):
         ax_copy(i).start()
@@ -427,34 +431,38 @@
         ring_a(1, i)
     wave_step(5)
     forward_x(0, 0)
-    for k in range(6, 9):
-        wave_step(k)
+    ring_b(2)
+    wave_step(6)
+    for i in range(XN):
+        ring_a(2, i)
+    for d in range(2):
+        forward_x(d, 1)
+    complete_x(0, 0)
+    wave_step(7)
+    wave_step(8)
     exchange_start(sb1, rb1, 0)
     acc[...] = jnp.zeros_like(acc)
     loads[5].wait()
     loads[6].wait()
 
-    @pl.loop(2, 8)
+    @pl.loop(3, 8)
     def _(k):
         ring_b(k)
         for i in range(XN):
             ring_a(k, i)
 
-            @pl.when(k >= 4)
-            def _():
+            if i == 0:
                 piece(k - 3, i)
+            else:
+
+                @pl.when(k >= 4)
+                def _():
+                    piece(k - 3, i)
 
         for d in range(2):
             forward_x(d, k - 1)
-
-        @pl.when(k == 2)
-        def _():
-            complete_x(0, 0)
-
-        @pl.when(k >= 3)
-        def _():
-            for d in range(2):
-                complete_x(d, k - 2)
+        for d in range(2):
+            complete_x(d, k - 2)
 
         @pl.when(k == ADAPT_AT)
         def _():
@@ -464,6 +472,10 @@
         def _():
             tiles()
 
+    piece(5, 0)
+    piece(5, 1)
+    for d in range(2):
+        forward_x(d, 7)
     for d in range(2):
         b_half_wait(d)
         for i in range(1, XN):
@@ -471,9 +483,6 @@
     for h in range(2):
         for d in range(2):
             a_wait(d, 8, 2 * d + h)
-        piece(5, h)
-    for d in range(2):
-        forward_x(d, 7)
     piece(5, 2)
     piece(5, 3)
     for d in range(2):
@@ -481,60 +490,46 @@
     block(6)
     for d in range(2):
         complete_x(d, 7)
-    block(7)
+    kv_piece(0, 7)
+    kv_piece(1, 7)
     for d in range(2):
         for i in range(1, XN):
             b8_wait(d, i)
-    block(8)
-    ig_ref[...] = (acc[...] + igl[...].astype(F32)).astype(BF)
+    kv_piece(0, 8)
+    for k in (7, 8):
+        for j in range(2):
+            ig_piece(k, j)
+    ig_ref[...] = (acc[...] + nn(back_t[...], d2t[...]).astype(BF).astype(F32)).astype(BF)
+    kvl = (2.0 * nn(low_t[...], up2[...])).astype(BF).astype(F32)
     exchange_wait(sb2, rb2, 1)
     got_ref[...] = rb2[...]
     ids_ref[...] = idx_ref[...]
 
-    total = own_kv[...]
-    for t in range(1, TN):
-        q = lax.rem(tp + t, TN)
-        remote(
-            rs_send.at[q], rs_recv.at[q], s_rs.at[q], r_rs.at[q], tp_device(q)
-        ).wait_recv()
-        total = total + rs_recv[q].astype(F32)
-    kv_ref[...] = (total + kvl[...].astype(F32)).astype(BF)
+    for h in range(2):
+        cols = slice(128 * h, 128 * h + 128)
+        total = own_kv[h]
+        for t in range(1, TN):
+            q = lax.rem(tp + t, TN)
+            remote(
+                rs_send.at[0], rs_recv.at[q, h], s_rs, r_rs.at[q, h], tp_device(q)
+            ).wait_recv()
+            total = total + rs_recv[q, h].astype(F32)
+        kv_ref[:, cols] = (total + kvl[:, cols]).astype(BF)
+
+    def drain(ref, sem):
+        remote(ref, ref, sem, s_loc.at[0], ring_device(0)).wait_send()
 
     exchange_drain(sb1, rb1, 0)
     exchange_drain(sb2, rb2, 1)
-    for i in range(1, XN):
-        ax_copy(i).wait_send()
-
-    @pl.loop(1, TN)
-    def _(t):
-        ar_copy(t).wait_send()
-        rs_copy(lax.rem(tp + t, TN)).wait_send()
-
-    for d in range(2):
-
-        @pl.loop(0, 7)
-        def _(k):
-            for xs in range(XN):
-                a_copy(d, k, xs).wait_send()
-            b_copy(d, k).wait_send()
-
-        for h in range(2):
-            a_copy(d, 7, 2 * d + h).wait_send()
-        b_half_copy(d).wait_send()
-    for d in range(2):
-        for i in range(1, XN):
-            b8_copy(d, i).wait_send()
-    for side in range(2):
-
-        @pl.loop(0, 8)
-        def _(k):
-            bx_copy(side, 0, k).wait_send()
-            bf_copy(side, 0, k).wait_send()
-
-        @pl.loop(1, 8)
-        def _(k):
-            bx_copy(side, 1, k).wait_send()
-            bf_copy(side, 1, k).wait_send()
+    drain(wa.at[0:96], s_ax)
+    drain(wb.at[0:96], s_b8)
+    drain(ar_recv.at[0 : TN - 1], s_ar)
+    drain(rs_send.at[0 : 2 * TN - 2], s_rs)
+    for d in range(2):
+        drain(wa.at[0:960], s_a.at[d])
+        drain(wb.at[0:240], s_b.at[d])
+        drain(wb.at[0:480], s_bx.at[d])
+        drain(wb.at[0:240], s_bf.at[d])
 
 
 def fused(tok, wt, cot, idx, dn, up):
@@ -554,11 +549,11 @@
             pltpu.VMEM((2048, LA), BF),
             pltpu.VMEM((2048, LB), BF),
             pltpu.VMEM((256, 1024), F32),
-            pltpu.VMEM((256, 256), F32),
-            pltpu.VMEM((TN, 256, 256), BF),
-            pltpu.VMEM((TN, 256, 256), BF),
-            pltpu.VMEM((256, 256), BF),
-            pltpu.VMEM((256, 1024), BF),
+            pltpu.VMEM((2, 256, 128), F32),
+            pltpu.VMEM((ZN, 256, 128), BF),
+            pltpu.VMEM((TN, 2, 256, 128), BF),
+            pltpu.VMEM((256, 32), BF),
+            pltpu.VMEM((256, 32), BF),
             pltpu.VMEM((256, 1024), BF),
             pltpu.VMEM((256, 2048), BF),
             pltpu.VMEM((2, FN), jnp.int32),
@@ -576,22 +571,22 @@
             pltpu.VMEM((32, 256), F32),
             pltpu.VMEM((TN, 32, 256), F32),
             pltpu.SemaphoreType.REGULAR((2, 9)),
-            dma((2, XN)),
+            dma(()),
             dma((2, XN)),
             dma((7,)),
-            dma((2, 8, XN)),
+            dma((2,)),
             dma((2, 9, XN)),
+            dma(()),
             dma((XN,)),
-            dma((XN,)),
-            dma((2, 8)),
+            dma((2,)),
             dma((2, 9)),
+            dma((2,)),
             dma((2, 16)),
+            dma((2,)),
             dma((2, 16)),
-            dma((2, 16)),
-            dma((2, 16)),
-            dma((TN,)),
-            dma((TN,)),
-            dma((TN,)),
+            dma(()),
+            dma((TN, 2)),
+            dma(()),
             dma((TN,)),
             dma((2,)),
             dma((2,)),

time: 76.7 us -> 64.1 us (0.84)
  the two profiles are of different devices: /device:TPU:16 before, /device:TPU:48 now
where the time goes in v3:
time: 64.1 us; the launch traced here: 64 us
  Pallas kernels  63.3 us (99%)
    pallas_call x1, Pallas kernels, fused(): pl.pallas_call(kernel, out_shape=(jax.ShapeDtypeStruct((256, 256), BF), j...  61.9 us
    pallas_call x1, Pallas kernels, fused(): pl.pallas_call(finish, out_shape=(jax.ShapeDtypeStruct((256, 256), BF), j...  1.45 us

profile of v3, /device:TPU:48, one launch (start us, length us, event | category | flops | bytes accessed | tf_op | source)
XLA Modules:
  0.0 64.0 jit_solution(11527497238583011286)
XLA Ops:
  0.6 61.9 %shard_map.93 = (bf16[256,256]{1,0:T(8,128)(2,1)S(1)}, bf16[256,1024]{1,0:T(8,128)(2,1)S(1)}, bf16[64,8,128]{2,1,0:T(8,128)(2,1)S(1)}, s32[2,64]{1,0:T(2,128)S(1)}) custom-call(bf16[256,1024]{1,0:T(8,128)(2,1)} %bitcast.14, bf16[32,1024]{1,0:T(8,128)(2,1)} %bitcast.16, bf16[256,2048]{1,0:T(8,128)(2,1)} %bitcast.13, s32[2,64]{1,0:T(2,128)} %idx_in.1, ...), custom_call_target="tpu_custom_call" | custom-call | tf_op jit(solution)/shard_map/pallas_call | solution.py:538
  62.5 1.5 %shard_map.94 = (bf16[256,256]{1,0:T(8,128)(2,1)}, bf16[256,1024]{1,0:T(8,128)(2,1)}, f32[256,512]{1,0:T(8,128)}, f32[16,4,512]{2,1,0:T(4,128)}) custom-call(bf16[256,256]{1,0:T(8,128)(2,1)S(1)} %get-tuple-element.12.kv_in, bf16[256,1024]{1,0:T(8,128)(2,1)S(1)} %get-tuple-element.13.ig_in, bf16[64,8,128]{2,1,0:T(8,128)(2,1)S(1)} %get-tuple-element.14.got_in, ...), custom_call_target="tpu_custom_call" | custom-call | tf_op jit(solution)/shard_map/pallas_call | solution.py:599

commit v4 on v3

--- a/solution.py
+++ b/solution.py
@@ -141,23 +141,23 @@
         sb32[:, 4 + m, :] = jnp.transpose(up)
 
     def exchange_start(src, dst, n):
-        own = pltpu.make_async_copy(src.at[f], dst.at[f], l_e.at[n])
+        own = pltpu.make_async_copy(src.at[f, 0:6], dst.at[f, 0:6], l_e.at[n])
         own.start()
 
         @pl.loop(1, FN, unroll=7)
         def _(p):
             q = lax.rem(f + p, FN)
-            remote(src.at[q], dst.at[f], s_e.at[n], r_e.at[n], plane_device(q)).start()
+            remote(src.at[q, 0:6], dst.at[f, 0:6], s_e.at[n], r_e.at[n], plane_device(q)).start()
 
     def exchange_wait(src, dst, n):
-        pltpu.make_async_copy(src.at[f], dst.at[f], l_e.at[n]).wait()
+        pltpu.make_async_copy(src.at[f, 0:6], dst.at[f, 0:6], l_e.at[n]).wait()
         remote(
-            src.at[0 : FN - 1], dst.at[0 : FN - 1], s_e.at[n], r_e.at[n], plane_device(f)
+            src.at[0 : FN - 1, 0:6], dst.at[0 : FN - 1, 0:6], s_e.at[n], r_e.at[n], plane_device(f)
         ).wait_recv()
 
     def exchange_drain(src, dst, n):
         remote(
-            src.at[0 : FN - 1], dst.at[0 : FN - 1], s_e.at[n], r_e.at[n], plane_device(f)
+            src.at[0 : FN - 1, 0:6], dst.at[0 : FN - 1, 0:6], s_e.at[n], r_e.at[n], plane_device(f)
         ).wait_send()
 
     def a_rows(d, k, xs):

time: 64.1 us -> 62.6 us (0.977)
  Pallas kernels: 63.3 us -> 61.8 us
    pallas_call x1, Pallas kernels: 61.9 us -> 60.4 us  [fused(): pl.pallas_call(kernel, out_shape=(jax.ShapeDtypeStruct((256, 256), BF), j...]
where the time goes in v4:
time: 62.6 us; the launch traced here: 62.5 us
  Pallas kernels  61.8 us (99%)
  between operations  0.64 us (1%)
    pallas_call x1, Pallas kernels, fused(): pl.pallas_call(kernel, out_shape=(jax.ShapeDtypeStruct((256, 256), BF), j...  60.4 us
    pallas_call x1, Pallas kernels, fused(): pl.pallas_call(finish, out_shape=(jax.ShapeDtypeStruct((256, 256), BF), j...  1.45 us

profile of v4, /device:TPU:48, one launch (start us, length us, event | category | flops | bytes accessed | tf_op | source)
XLA Modules:
  0.0 62.5 jit_solution(2653305046614844128)
XLA Ops:
  0.6 60.4 %shard_map.93 = (bf16[256,256]{1,0:T(8,128)(2,1)S(1)}, bf16[256,1024]{1,0:T(8,128)(2,1)S(1)}, bf16[64,8,128]{2,1,0:T(8,128)(2,1)S(1)}, s32[2,64]{1,0:T(2,128)S(1)}) custom-call(bf16[256,1024]{1,0:T(8,128)(2,1)} %bitcast.14, bf16[32,1024]{1,0:T(8,128)(2,1)} %bitcast.16, bf16[256,2048]{1,0:T(8,128)(2,1)} %bitcast.13, s32[2,64]{1,0:T(2,128)} %idx_in.1, ...), custom_call_target="tpu_custom_call" | custom-call | tf_op jit(solution)/shard_map/pallas_call | solution.py:538
  61.0 1.4 %shard_map.94 = (bf16[256,256]{1,0:T(8,128)(2,1)}, bf16[256,1024]{1,0:T(8,128)(2,1)}, f32[256,512]{1,0:T(8,128)}, f32[16,4,512]{2,1,0:T(4,128)}) custom-call(bf16[256,256]{1,0:T(8,128)(2,1)S(1)} %get-tuple-element.12.kv_in, bf16[256,1024]{1,0:T(8,128)(2,1)S(1)} %get-tuple-element.13.ig_in, bf16[64,8,128]{2,1,0:T(8,128)(2,1)S(1)} %get-tuple-element.14.got_in, ...), custom_call_target="tpu_custom_call" | custom-call | tf_op jit(solution)/shard_map/pallas_call | solution.py:599
